TPU v7x, 32 devices: a whole 2x2x4 slice. The times are simulated.
32 devices in a mesh: dp: 4 (over x, core), fsdp: 4 (over z), mp: 2 (over y).
Axes of the slice: x: 2, y: 2, z: 4, core: 2. Of those that a mesh axis runs over, the one named last changes fastest.
Arguments:
- tokens_in: bfloat16 [4096, 3072], P(('dp', 'fsdp', 'mp')), may hold values from -40 to 40
- segment_ids: int32 [4096], P(('dp', 'fsdp', 'mp')), may hold values from 0 to 31, never falling along the last dimension, each value on 1 to 512 neighbouring positions
- target_ids: int32 [4096], P(('dp', 'fsdp', 'mp')), may hold values from 0 to 8191
- old_weights: bfloat16 [4, 3072, 2048], P(None, ('dp', 'fsdp', 'mp'))
- old_first: float32 [4, 3072, 2048], P(None, ('dp', 'fsdp', 'mp')), may hold values from -6 to 6
- old_second: float32 [4, 3072, 2048], P(None, ('dp', 'fsdp', 'mp')), may hold values from 0.01 to 4
- old_block: int32 [32], P(('dp', 'fsdp', 'mp')), may hold values from 0 to 31, each once
- new_residue: int32 [4], P('dp'), may hold values from 0 to 3, each once
- norm_gain: float32 [3072], replicated, may hold values from 0.5 to 1.5
- head_weight: bfloat16 [3072, 8192], P(None, ('fsdp', 'mp'))
Outputs:
- new_weights: bfloat16 [4, 3072, 2048], P(None, 'dp', ('fsdp', 'mp'))
- new_first: float32 [4, 3072, 2048], P(None, 'dp', ('fsdp', 'mp'))
- new_second: float32 [4, 3072, 2048], P(None, 'dp', ('fsdp', 'mp'))
- loss: float32 [4096], P(('dp', 'fsdp', 'mp'))
Inputs may be any that keep to these rules, and one draw needn't show every extreme that they name: `old_block`: a permutation of the old layout's row blocks. `new_residue`: a permutation; index i of dp holds the rows whose number modulo 4 is new_residue[i], in rising order. `segment_ids`: never falling along the tokens.
All inputs are finite; a program needn't handle non-finite values.
Results may differ from a plain program's by a relative error of at most 0.0075.
Values may be sent and summed in bfloat16 or wider, within the bound.
A program may use at most 192 MiB of HBM per device.

v0:
```python
import math
import jax
import jax.numpy as jnp
from jax import lax
from jax.sharding import PartitionSpec as P

HD = 128


def inverse_of(table):
    total_count = table.shape[0]
    places = jnp.arange(total_count, dtype=jnp.int32)
    return jnp.sum(jnp.where(table[None, :] == places[:, None], places[None, :], 0), axis=1)


def pack_rows(stored, residues, fm_count):
    matrices, row_count, columns = stored.shape
    dp_count = residues.shape[0]
    split_rows = stored.reshape(
        matrices, row_count // dp_count, dp_count, fm_count, columns // fm_count
    )
    chosen = jnp.take(split_rows, residues, axis=2, mode="clip")
    return chosen.transpose(2, 3, 0, 1, 4).reshape(
        dp_count * fm_count, matrices, row_count // dp_count, columns // fm_count
    )


def unpack_rows(received, holder):
    ordered = jnp.take(received, holder, axis=0, mode="clip")
    devices, matrices, pair_rows, group_cols = ordered.shape
    return ordered.transpose(1, 0, 2, 3).reshape(matrices, devices * pair_rows, group_cols)


def norm_rows(hidden, norm_gain):
    scale = lax.rsqrt(jnp.mean(hidden * hidden, axis=1, keepdims=True) + 1e-05)
    return (hidden * scale * norm_gain).astype(jnp.bfloat16)


FLAGS = dict(tail="a2a", first="before_rs", second="free", tokens="first")


def share_tables(segment_ids, target_ids, old_block, new_residue):
    axes = ("dp", "fsdp", "mp")
    own = jnp.concatenate([segment_ids, target_ids, old_block, new_residue])
    rows = jnp.broadcast_to(own[None, None], (lax.axis_size(axes), 1, own.shape[0]))
    rows = lax.all_to_all(rows, axes, split_axis=0, concat_axis=0, tiled=True)[:, 0]
    count = segment_ids.shape[0]
    fm_count = lax.axis_size(("fsdp", "mp"))
    here = lax.dynamic_slice_in_dim(rows, lax.axis_index("dp") * fm_count, fm_count)
    segments = here[:, :count].reshape(-1)
    targets = here[:, count : 2 * count].reshape(-1)
    return (segments, targets, rows[:, 2 * count], rows[::fm_count, 2 * count + 1])


def joint_loss(row_top, row_total, picked):
    axes = ("fsdp", "mp")
    fm_count = lax.axis_size(axes)
    parts = jnp.stack([row_top, row_total, picked])
    own_count = parts.shape[1] // fm_count
    if FLAGS["tail"] == "a2a":
        parts = parts.reshape(3, fm_count, own_count).transpose(1, 0, 2)
        parts = lax.all_to_all(parts, axes, split_axis=0, concat_axis=0, tiled=True)
    else:
        place = lax.axis_index(axes)
        rows = jnp.zeros((fm_count,) + parts.shape, jnp.float32)
        rows = lax.psum(lax.dynamic_update_slice(rows, parts[None], (place, 0, 0)), axes)
        parts = lax.dynamic_slice_in_dim(rows, place * own_count, own_count, axis=2)
    tops, totals, targets = (parts[:, 0], parts[:, 1], parts[:, 2])
    joint_max = jnp.max(tops, axis=0)
    joint_total = jnp.sum(totals * jnp.exp(tops - joint_max[None]), axis=0)
    return joint_max + jnp.log(joint_total) - jnp.sum(targets, axis=0)


def body(
    tokens_in,
    segment_ids,
    target_ids,
    old_weights,
    old_first,
    old_second,
    old_block,
    new_residue,
    norm_gain,
    head_weight,
):
    dp_count = lax.axis_size("dp")
    fm_count = lax.axis_size(("fsdp", "mp"))
    everyone = ("dp", "fsdp", "mp")
    columns = old_weights.shape[2]
    group_cols = columns // fm_count
    model_width = tokens_in.shape[1]
    new_rows = model_width // dp_count
    segments, targets, table_all, residues = share_tables(
        segment_ids, target_ids, old_block, new_residue
    )
    holder = inverse_of(table_all)
    inverse_res = inverse_of(residues)
    feature_ids = (
        residues[:, None] + dp_count * jnp.arange(new_rows, dtype=jnp.int32)[None]
    ).reshape(-1)
    logical_ids = (
        jnp.arange(new_rows, dtype=jnp.int32)[:, None] + new_rows * inverse_res[None]
    ).reshape(-1)
    own_picked = jnp.take(tokens_in, feature_ids, axis=1, mode="clip")
    picked_cols = lax.all_gather(own_picked, ("fsdp", "mp"), axis=0, tiled=True)
    seq_len = picked_cols.shape[0]
    weights_sent = pack_rows(old_weights, residues, fm_count)
    weights_got = lax.all_to_all(weights_sent, everyone, split_axis=0, concat_axis=0, tiled=True)
    first_sent = pack_rows(old_first, residues, fm_count)
    second_sent = pack_rows(old_second, residues, fm_count)
    if FLAGS["first"] != "free":
        weights_got, first_sent, second_sent = lax.optimization_barrier(
            (weights_got, first_sent, second_sent)
        )
    new_weights = unpack_rows(weights_got, holder)
    projections = new_weights[:3]
    if FLAGS.get("tokens") == "first":
        picked_cols, projections, first_sent = lax.optimization_barrier(
            (picked_cols, projections, first_sent)
        )
    first_got = lax.all_to_all(first_sent, everyone, split_axis=0, concat_axis=0, tiled=True)
    piece = lax.all_gather(projections, "dp", axis=1, tiled=True)
    projected = jnp.einsum("sr,mrc->msc", picked_cols, piece, preferred_element_type=jnp.float32)
    heads = group_cols // HD
    queries = projected[0].astype(jnp.bfloat16).reshape(seq_len, heads, HD)
    keys_all = projected[1].astype(jnp.bfloat16).reshape(seq_len, heads, HD)
    values_all = projected[2].astype(jnp.bfloat16).reshape(seq_len, heads, HD)
    positions_all = jnp.arange(seq_len, dtype=jnp.int32)
    allowed = (positions_all[:, None] >= positions_all[None, :]) & (
        segments[:, None] == segments[None, :]
    )
    scores = jnp.einsum("shd,thd->hst", queries, keys_all, preferred_element_type=jnp.float32) * (
        1.0 / math.sqrt(HD)
    )
    scores = jnp.where(allowed[None], scores, -1e30)
    row_max = jnp.max(scores, axis=2, keepdims=True)
    expo = jnp.where(allowed[None], jnp.exp(scores - row_max), 0.0)
    soft = (expo / jnp.sum(expo, axis=2, keepdims=True)).astype(jnp.bfloat16)
    attended = jnp.einsum("hst,thd->shd", soft, values_all, preferred_element_type=jnp.float32)
    attended = attended.astype(jnp.bfloat16).reshape(seq_len, group_cols)
    shuffled = jnp.einsum(
        "sc,rc->sr",
        attended,
        lax.all_gather(new_weights[3], "dp", axis=0, tiled=True),
        preferred_element_type=jnp.float32,
    )
    partial_value = shuffled.astype(jnp.bfloat16)
    if FLAGS["first"] == "rs_first":
        partial_value, second_sent = lax.optimization_barrier((partial_value, second_sent))
    if FLAGS["first"] == "before_rs":
        partial_value, first_got, second_sent = lax.optimization_barrier(
            (partial_value, first_got, second_sent)
        )
    second_got = lax.all_to_all(second_sent, everyone, split_axis=0, concat_axis=0, tiled=True)
    own_sum = lax.psum_scatter(partial_value, ("fsdp", "mp"), scatter_dimension=0, tiled=True)
    own_sum = jnp.take(own_sum, logical_ids, axis=1, mode="clip").astype(jnp.float32)
    own_normed = norm_rows(tokens_in.astype(jnp.float32) + own_sum, norm_gain)
    if FLAGS["second"] == "before_ag":
        own_normed, second_got = lax.optimization_barrier((own_normed, second_got))
    new_first = unpack_rows(first_got, holder)
    new_second = unpack_rows(second_got, holder)
    normed = lax.all_gather(own_normed, ("fsdp", "mp"), axis=0, tiled=True)
    logits = jnp.dot(normed, head_weight, preferred_element_type=jnp.float32)
    vocab_dev = logits.shape[1]
    offset = lax.axis_index(("fsdp", "mp")) * vocab_dev
    row_top = jnp.max(logits, axis=1)
    row_total = jnp.sum(jnp.exp(logits - row_top[:, None]), axis=1)
    vocab_ids = jnp.arange(vocab_dev, dtype=jnp.int32) + offset
    picked = jnp.sum(jnp.where(vocab_ids[None, :] == targets[:, None], logits, 0.0), axis=1)
    loss = joint_loss(row_top, row_total, picked)
    return (new_weights, new_first, new_second, loss)


def solution(mesh):
    placed = (
        P(("dp", "fsdp", "mp"), None),
        P(("dp", "fsdp", "mp")),
        P(("dp", "fsdp", "mp")),
        P(None, ("dp", "fsdp", "mp"), None),
        P(None, ("dp", "fsdp", "mp"), None),
        P(None, ("dp", "fsdp", "mp"), None),
        P(("dp", "fsdp", "mp")),
        P("dp"),
        P(),
        P(None, ("fsdp", "mp")),
    )
    return jax.shard_map(
        body,
        mesh=mesh,
        in_specs=placed,
        out_specs=(
            P(None, "dp", ("fsdp", "mp")),
            P(None, "dp", ("fsdp", "mp")),
            P(None, "dp", ("fsdp", "mp")),
            P(("dp", "fsdp", "mp")),
        ),
        check_vma=False,
    )
```

profile of v0, /device:TPU:0, one launch (start us, length us, event | category | flops | bytes accessed | tf_op | source)
XLA Modules:
  0.0 589.0 jit_solution(5896758327097351042)
XLA Ops:
  9.9 7.3 %all-to-all-start = ((s32[32,1,258]{2,1,0:T(1,128)}), s32[32,1,258]{2,1,0:T(1,128)S(1)}, u32[]{:S(2)}, u32[]{:S(2)}) async-start(s32[32,1,258]{2,1,0:T(1,128)} %broadcast_in_dim.85), calls=%async_computation | async-start | bytes 98304 | tf_op jit(solution)/shard_map/all_to_all | solution.py:46
  18.8 5.7 all-to-all-done
  24.7 11.4 %gather_fusion.4 = bf16[3072,128]{1,0:T(8,128)(2,1)} fusion(bf16[128,3072]{0,1:T(8,128)(2,1)S(1)} %copy.84, s32[3072]{0:T(1024)S(1)} %broadcast_clamp_fusion.1), kind=kCustom, calls=%fused_computation.4 | custom fusion | bytes 1585152 | tf_op jit(solution)/shard_map/jit(_take)/gather | solution.py:104
  45.9 5.1 copy.105
  54.2 4.3 gather_fusion.1
  58.5 4.5 copy.81
  63.0 4.4 gather_fusion.2
  67.4 4.6 copy.82
  72.2 34.0 %all-to-all-done.1 = bf16[32,4,24,256]{3,2,1,0:T(8,128)(2,1)S(1)} async-done(((bf16[32,4,24,256]{3,2,1,0:T(8,128)(2,1)}), bf16[32,4,24,256]{3,2,1,0:T(8,128)(2,1)S(1)}, u32[]{:S(2)}, u32[]{:S(2)}) %all-to-all-start.1) | async-done | bytes 1572896 | tf_op jit(solution)/shard_map/all_to_all | solution.py:108
  109.7 50.7 %all-gather.12.cloned.1.call-done = bf16[1024,3072]{0,1:T(8,128)(2,1)} async-done(((bf16[128,3072]{0,1:T(8,128)(2,1)}), bf16[1024,3072]{0,1:T(8,128)(2,1)}) %all-gather.12.cloned.1.call-update) | async-done | bytes 6291472 | tf_op jit(solution)/shard_map/all_gather | solution.py:105
  167.9 56.2 %all-gather.6.cloned.1.call-done = bf16[3,3072,256]{1,2,0:T(8,128)(2,1)} async-done(((bf16[3,768,256]{1,2,0:T(8,128)(2,1)}), bf16[3,3072,256]{1,2,0:T(8,128)(2,1)}) %all-gather.6.cloned.1.call-update) | async-done | bytes 4718608 | tf_op jit(solution)/shard_map/all_gather | solution.py:122
  224.1 8.5 %fusion.12 = bf16[3,1024,256]{1,2,0:T(8,128)(2,1)S(1)} fusion(bf16[3,3072,256]{1,2,0:T(8,128)(2,1)} %all-gather.6.cloned.1.call-done, bf16[1024,3072]{0,1:T(8,128)(2,1)} %all-gather.12.cloned.1.call-done), kind=kOutput, calls=%fused_computation.28 | convolution fusion | flops 4832624640 | bytes 12582912 | tf_op jit(solution)/shard_map/sr,mrc->msc/dot_general | solution.py:123
  233.9 8.7 %fusion.22 = (f32[2,1024]{1,0:T(2,128)S(1)}, f32[2,1024,1024]{1,2,0:T(8,128)}) fusion(pred[1024,1024]{0,1:T(8,128)(4,1)S(1)} %fusion.6, bf16[1024,2,128]{0,2,1:T(8,128)(2,1)} %bitcast.102, bf16[1024,2,128]{0,2,1:T(8,128)(2,1)} %bitcast.101), kind=kOutput, calls=%fused_computation.60 | convolution fusion | flops 547357696 | bytes 10493952 | tf_op jit(solution)/shard_map/sub | solution.py:137
  242.5 4.3 fusion.15
  250.7 5.9 %convolution_convert_fusion = bf16[1024,3072]{1,0:T(8,128)(2,1)} fusion(bf16[1024,256]{0,1:T(8,128)(2,1)S(1)} %bitcast.99, bf16[3072,256]{1,0:T(8,128)(2,1)} %all-gather.8.cloned.1.call-done), kind=kOutput, calls=%fused_computation.15 | convolution fusion | flops 1613758464 | bytes 8388608 | tf_op jit(solution)/shard_map/sc,rc->sr/dot_general | solution.py:141
  257.1 119.5 %reduce-scatter.2.cloned.1.call-done = bf16[128,3072]{1,0:T(8,128)(2,1)} async-done(((bf16[1024,3072]{1,0:T(8,128)(2,1)}), bf16[128,3072]{1,0:T(8,128)(2,1)}) %reduce-scatter.2.cloned.1.call-update) | async-done | bytes 786448 | tf_op jit(solution)/shard_map/reduce_scatter | solution.py:155
  378.0 11.5 %gather_fusion.7 = bf16[3072,128]{1,0:T(8,128)(2,1)} fusion(bf16[128,3072]{0,1:T(8,128)(2,1)S(1)} %copy.94, s32[3072]{0:T(1024)S(1)} %broadcast_clamp_fusion), kind=kCustom, calls=%fused_computation.7 | custom fusion | bytes 1585152 | tf_op jit(solution)/shard_map/jit(_take)/gather | solution.py:156
  393.7 4.2 all-to-all-start.3
  397.9 149.0 %all-gather.10.cloned.1.call-done = bf16[1024,3072]{0,1:T(8,128)(2,1)} async-done(((bf16[128,3072]{0,1:T(8,128)(2,1)}), bf16[1024,3072]{0,1:T(8,128)(2,1)}) %all-gather.10.cloned.1.call-update) | async-done | bytes 6291472 | tf_op jit(solution)/shard_map/all_gather | solution.py:162
  546.9 10.7 %fusion.23 = (f32[1024]{0:T(1024)S(1)}, f32[1024,1024]{0,1:T(8,128)S(1)}) fusion(bf16[1024,3072]{0,1:T(8,128)(2,1)} %all-gather.10.cloned.1.call-done, bf16[3072,1024]{1,0:T(8,128)(2,1)} %param.19), kind=kOutput, calls=%fused_computation.61 | convolution fusion | flops 6443498496 | bytes 16781312 | tf_op jit(solution)/shard_map/dot_general | solution.py:163
  559.7 4.7 all-to-all-start.4
  565.6 4.3 gather_fusion.5
  569.9 3.9 copy.91
  573.8 4.3 gather_fusion.6
  (70 shorter events, 45.9 us)
Async XLA Ops:
  9.9 14.6 %all-to-all-start = ((s32[32,1,258]{2,1,0:T(1,128)}), s32[32,1,258]{2,1,0:T(1,128)S(1)}, u32[]{:S(2)}, u32[]{:S(2)}) async-start(s32[32,1,258]{2,1,0:T(1,128)} %broadcast_in_dim.85), calls=%async_computation | async-start | bytes 98304 | tf_op jit(solution)/shard_map/all_to_all | solution.py:46
  17.2 143.2 %all-gather.12.cloned.1.call-start = ((), (), s32[]{:S(2)}) async-start(), calls=%async_computation.10 | async-start | bytes 7077888 | tf_op jit(solution)/shard_map/all_gather | solution.py:105
  24.4 11.8 %copy-start.2 = (s32[32,1,258]{2,1,0:T(1,128)}, s32[32,1,258]{2,1,0:T(1,128)S(1)}, u32[]{:S(2)}) copy-start(s32[32,1,258]{2,1,0:T(1,128)S(1)} %all-to-all-done) | copy-start | bytes 99076
  43.2 63.1 %all-to-all-start.1 = ((bf16[32,4,24,256]{3,2,1,0:T(8,128)(2,1)}), bf16[32,4,24,256]{3,2,1,0:T(8,128)(2,1)S(1)}, u32[]{:S(2)}, u32[]{:S(2)}) async-start(bf16[32,4,24,256]{3,2,1,0:T(8,128)(2,1)} %bitcast.1), calls=%async_computation.1 | async-start | bytes 3145728 | tf_op jit(solution)/shard_map/all_to_all | solution.py:108
  45.9 178.3 %all-gather.6.cloned.1.call-start = ((), (), s32[]{:S(2)}) async-start(), calls=%async_computation.6 | async-start | bytes 5898240 | tf_op jit(solution)/shard_map/all_gather | solution.py:122
  45.9 5.1 copy-start.1
  106.3 1.1 copy-start
  161.9 94.7 %all-to-all-start.2 = ((f32[32,4,24,256]{3,2,1,0:T(8,128)}), f32[32,4,24,256]{3,2,1,0:T(8,128)}, u32[]{:S(2)}, u32[]{:S(2)}) async-start(f32[32,4,24,256]{3,2,1,0:T(8,128)} %bitcast.81), calls=%async_computation.2 | async-start | bytes 6291456 | tf_op jit(solution)/shard_map/all_to_all | solution.py:121
  165.5 85.2 %all-gather.8.cloned.1.call-start = ((), (), s32[]{:S(2)}) async-start(), calls=%async_computation.7 | async-start | bytes 1966080 | tf_op jit(solution)/shard_map/all_gather | solution.py:144
  167.7 208.8 %reduce-scatter.2.cloned.1.call-start = ((), (), s32[]{:S(2)}) async-start(), calls=%async_computation.8 | async-start | bytes 7077888 | tf_op jit(solution)/shard_map/reduce_scatter | solution.py:155
  256.6 290.3 %all-gather.10.cloned.1.call-start = ((), (), s32[]{:S(2)}) async-start(), calls=%async_computation.9 | async-start | bytes 7077888 | tf_op jit(solution)/shard_map/all_gather | solution.py:162
  378.0 13.1 %copy-start.3 = (f32[3072]{0:T(1024)S(1)}, f32[3072]{0:T(1024)}, u32[]{:S(2)}) copy-start(f32[3072]{0:T(1024)} %param.18) | copy-start | bytes 36868
  393.7 166.0 %all-to-all-start.3 = ((f32[32,4,24,256]{3,2,1,0:T(8,128)}), f32[32,4,24,256]{3,2,1,0:T(8,128)}, u32[]{:S(2)}, u32[]{:S(2)}) async-start(f32[32,4,24,256]{3,2,1,0:T(8,128)} %bitcast.80), calls=%async_computation.3 | async-start | bytes 6291456 | tf_op jit(solution)/shard_map/all_to_all | solution.py:154
  559.7 22.3 %all-to-all-start.4 = ((f32[8,3,128]{2,1,0:T(4,128)}), f32[8,3,128]{2,1,0:T(4,128)S(1)}, u32[]{:S(2)}, u32[]{:S(2)}) async-start(f32[8,3,128]{2,1,0:T(4,128)} %maximum_bitcast_fusion), calls=%async_computation.5 | async-start | bytes 32768 | tf_op jit(solution)/shard_map/all_to_all | solution.py:62
Sparse Core Ops, SparseCore 0:
  36.3 124.0 all-gather.11
  162.5 61.5 all-gather.5
  225.7 24.9 all-gather.7
  256.7 119.7 reduce-scatter.1
  393.8 153.0 all-gather.9
where the time goes:
time: 590 us; the launch traced here: 589 us
  waiting for transfers between devices  419 us (71%)
  local copies, waits for them, and re-layouts  85.3 us (14%)
  matrix products  38.1 us (6%)
  starting transfers between devices  22.9 us (4%)
  between operations  15.3 us (3%)
  other arithmetic  8.52 us (1%)
    all_gather x1, waiting for transfers between devices, body(): normed = lax.all_gather(own_normed, ('fsdp', 'mp'), axis=0, tiled=True)  149 us
    reduce_scatter x1, waiting for transfers between devices, body(): lax.psum_scatter(partial_value, ('fsdp', 'mp'), scatter_dimension=0, tile...  119 us
    all_gather x1, waiting for transfers between devices, body(): piece = lax.all_gather(projections, 'dp', axis=1, tiled=True)  56.2 us
    all_gather x1, waiting for transfers between devices, body(): picked_cols = lax.all_gather(own_picked, ('fsdp', 'mp'), axis=0, tiled=True)  50.7 us
    all_to_all x1, waiting for transfers between devices, body(): lax.all_to_all(weights_sent, everyone, split_axis=0, concat_axis=0, tiled...  34 us
    unnamed x14, local copies, waits for them, and re-layouts  12.8 us
    transpose x3, local copies, waits for them, and re-layouts, pack_rows(): chosen.transpose(2, 3, 0, 1, 4)  12.3 us
  transfers between devices with their start and end apart: 10, of which 7 were waited for; matrix products, arithmetic and copies ran while one was open for 17% of the time, Pallas kernels for 0%

commit v1 on v0

--- a/solution.py
+++ b/solution.py
@@ -119,8 +119,21 @@
             (picked_cols, projections, first_sent)
         )
     first_got = lax.all_to_all(first_sent, everyone, split_axis=0, concat_axis=0, tiled=True)
-    piece = lax.all_gather(projections, "dp", axis=1, tiled=True)
-    projected = jnp.einsum("sr,mrc->msc", picked_cols, piece, preferred_element_type=jnp.float32)
+    size, index, width = (lax.axis_size("dp"), lax.axis_index("dp"), projections.shape[1])
+    right = [(i, (i + 1) % size) for i in range(size)]
+    held, projected = (projections, None)
+    for step in range(size):
+        following = lax.ppermute(held, "dp", right) if step < size - 1 else None
+        update = jnp.einsum(
+            "sr,mrc->msc",
+            lax.dynamic_slice_in_dim(
+                picked_cols, (index - step) % size * width, held.shape[1], axis=1
+            ),
+            held,
+            preferred_element_type=jnp.float32,
+        )
+        projected = update if projected is None else projected + update
+        held = following
     heads = group_cols // HD
     queries = projected[0].astype(jnp.bfloat16).reshape(seq_len, heads, HD)
     keys_all = projected[1].astype(jnp.bfloat16).reshape(seq_len, heads, HD)

time: 590 us -> 602 us (1.020)
    ppermute x0 -> x3, waiting for transfers between devices: none -> 67.3 us  [body(): following = lax.ppermute(held, 'dp', right) if step < size - 1 else None]
    all_gather x1 -> x0, waiting for transfers between devices: 56.2 us -> none  [body(): piece = lax.all_gather(projections, 'dp', axis=1, tiled=True)]
    dot_general x1 -> x4, matrix products: 8.53 us -> 12.5 us  [body(): jnp.einsum('sr,mrc->msc', lax.dynamic_slice_in_dim(picked_cols, (index -...]
    unnamed x14 -> x16, local copies, waits for them, and re-layouts: 12.8 us -> 13.7 us
  transfers between devices with their start and end apart: 10 -> 12, of which waited for: 7 -> 8; matrix products, arithmetic and copies ran while one was open for 17% -> 17% of each run, Pallas kernels for 0% -> 0%
where the time goes in v1:
time: 602 us; the launch traced here: 601 us
  waiting for transfers between devices  425 us (71%)
  local copies, waits for them, and re-layouts  85 us (14%)
  matrix products  42.1 us (7%)
  starting transfers between devices  22.8 us (4%)
  between operations  16.7 us (3%)
  other arithmetic  9.49 us (2%)
    all_gather x1, waiting for transfers between devices, body(): normed = lax.all_gather(own_normed, ('fsdp', 'mp'), axis=0, tiled=True)  149 us
    reduce_scatter x1, waiting for transfers between devices, body(): lax.psum_scatter(partial_value, ('fsdp', 'mp'), scatter_dimension=0, tile...  119 us
    ppermute x3, waiting for transfers between devices, body(): following = lax.ppermute(held, 'dp', right) if step < size - 1 else None  67.3 us
    all_gather x1, waiting for transfers between devices, body(): picked_cols = lax.all_gather(own_picked, ('fsdp', 'mp'), axis=0, tiled=True)  49.4 us
    all_to_all x1, waiting for transfers between devices, body(): lax.all_to_all(weights_sent, everyone, split_axis=0, concat_axis=0, tiled...  33.9 us
    unnamed x16, local copies, waits for them, and re-layouts  13.7 us
    dot_general x4, matrix products, body(): jnp.einsum('sr,mrc->msc', lax.dynamic_slice_in_dim(picked_cols, (index -...  12.5 us
    transpose x3, local copies, waits for them, and re-layouts, pack_rows(): chosen.transpose(2, 3, 0, 1, 4)  12.3 us
  transfers between devices with their start and end apart: 12, of which 8 were waited for; matrix products, arithmetic and copies ran while one was open for 17% of the time, Pallas kernels for 0%

profile of v1, /device:TPU:0, one launch (start us, length us, event | category | flops | bytes accessed | tf_op | source)
XLA Modules:
  0.0 600.8 jit_solution(17647871988592214942)
XLA Ops:
  10.7 7.3 %all-to-all-start = ((s32[32,1,258]{2,1,0:T(1,128)}), s32[32,1,258]{2,1,0:T(1,128)S(1)}, u32[]{:S(2)}, u32[]{:S(2)}) async-start(s32[32,1,258]{2,1,0:T(1,128)} %broadcast_in_dim.85), calls=%async_computation | async-start | bytes 98304 | tf_op jit(solution)/shard_map/all_to_all | solution.py:46
  19.6 5.7 all-to-all-done
  25.9 9.1 %gather_fusion.4 = bf16[3072,128]{1,0:T(8,128)(2,1)S(1)} fusion(bf16[128,3072]{0,1:T(8,128)(2,1)S(1)} %copy.88, s32[3072]{0:T(1024)S(1)} %broadcast_clamp_fusion.1), kind=kCustom, calls=%fused_computation.4 | custom fusion | bytes 1585152 | tf_op jit(solution)/shard_map/jit(_take)/gather | solution.py:104
  45.9 5.1 copy.109
  54.2 4.3 gather_fusion.1
  58.5 4.5 copy.85
  63.1 4.3 gather_fusion.2
  67.4 4.6 copy.86
  72.2 33.9 %all-to-all-done.1 = bf16[32,4,24,256]{3,2,1,0:T(8,128)(2,1)S(1)} async-done(((bf16[32,4,24,256]{3,2,1,0:T(8,128)(2,1)}), bf16[32,4,24,256]{3,2,1,0:T(8,128)(2,1)S(1)}, u32[]{:S(2)}, u32[]{:S(2)}) %all-to-all-start.1) | async-done | bytes 1572896 | tf_op jit(solution)/shard_map/all_to_all | solution.py:108
  109.6 49.4 %all-gather.9.cloned.1.call-done = bf16[1024,3072]{1,0:T(8,128)(2,1)} async-done(((bf16[128,3072]{1,0:T(8,128)(2,1)}), bf16[1024,3072]{1,0:T(8,128)(2,1)}) %all-gather.9.cloned.1.call-update) | async-done | bytes 6291472 | tf_op jit(solution)/shard_map/all_gather | solution.py:105
  164.1 28.9 %collective-permute-done = bf16[3,768,256]{1,2,0:T(8,128)(2,1)} collective-permute-done((bf16[3,768,256]{1,2,0:T(8,128)(2,1)}, bf16[3,768,256]{1,2,0:T(8,128)(2,1)}, u32[]{:S(2)}, u32[]{:S(2)}) %collective-permute-start) | collective-permute-done | bytes 1179680 | tf_op jit(solution)/shard_map/ppermute | solution.py:126
  193.8 23.5 %collective-permute-done.1 = bf16[3,768,256]{1,2,0:T(8,128)(2,1)} collective-permute-done((bf16[3,768,256]{1,2,0:T(8,128)(2,1)}, bf16[3,768,256]{1,2,0:T(8,128)(2,1)}, u32[]{:S(2)}, u32[]{:S(2)}) %collective-permute-start.1) | collective-permute-done | bytes 1179680 | tf_op jit(solution)/shard_map/ppermute | solution.py:126
  229.2 14.8 %collective-permute-done.2 = bf16[3,768,256]{1,2,0:T(8,128)(2,1)} collective-permute-done((bf16[3,768,256]{1,2,0:T(8,128)(2,1)}, bf16[3,768,256]{1,2,0:T(8,128)(2,1)}, u32[]{:S(2)}, u32[]{:S(2)}) %collective-permute-start.2) | collective-permute-done | bytes 1179680 | tf_op jit(solution)/shard_map/ppermute | solution.py:126
  249.1 8.7 %fusion.32 = (f32[2,1024]{1,0:T(2,128)S(1)}, f32[2,1024,1024]{1,2,0:T(8,128)}) fusion(pred[1024,1024]{0,1:T(8,128)(4,1)S(1)} %copy-done.2, bf16[1024,2,128]{0,2,1:T(8,128)(2,1)} %bitcast.113, bf16[1024,2,128]{0,2,1:T(8,128)(2,1)} %bitcast.112), kind=kOutput, calls=%fused_computation.73 | convolution fusion | flops 547357696 | bytes 10493952 | tf_op jit(solution)/shard_map/sub | solution.py:150
  257.7 4.3 fusion.21
  262.1 5.9 convolution_convert_fusion
  268.7 119.0 %reduce-scatter.2.cloned.1.call-done = bf16[128,3072]{1,0:T(8,128)(2,1)} async-done(((bf16[1024,3072]{1,0:T(8,128)(2,1)}), bf16[128,3072]{1,0:T(8,128)(2,1)}) %reduce-scatter.2.cloned.1.call-update) | async-done | bytes 786448 | tf_op jit(solution)/shard_map/reduce_scatter | solution.py:168
  389.2 11.5 %gather_fusion.7 = bf16[3072,128]{1,0:T(8,128)(2,1)} fusion(bf16[128,3072]{0,1:T(8,128)(2,1)S(1)} %copy.99, s32[3072]{0:T(1024)S(1)} %broadcast_clamp_fusion), kind=kCustom, calls=%fused_computation.7 | custom fusion | bytes 1585152 | tf_op jit(solution)/shard_map/jit(_take)/gather | solution.py:169
  404.9 4.0 all-to-all-start.3
  408.9 149.2 %all-gather.7.cloned.1.call-done = bf16[1024,3072]{0,1:T(8,128)(2,1)} async-done(((bf16[128,3072]{0,1:T(8,128)(2,1)}), bf16[1024,3072]{0,1:T(8,128)(2,1)}) %all-gather.7.cloned.1.call-update) | async-done | bytes 6291472 | tf_op jit(solution)/shard_map/all_gather | solution.py:175
  558.1 10.7 %fusion.33 = (f32[1024]{0:T(1024)S(1)}, f32[1024,1024]{0,1:T(8,128)S(1)}) fusion(bf16[1024,3072]{0,1:T(8,128)(2,1)} %all-gather.7.cloned.1.call-done, bf16[3072,1024]{1,0:T(8,128)(2,1)} %param.19), kind=kOutput, calls=%fused_computation.74 | convolution fusion | flops 6443498496 | bytes 16781312 | tf_op jit(solution)/shard_map/dot_general | solution.py:176
  570.8 4.7 all-to-all-start.4
  576.8 4.3 gather_fusion.5
  584.9 4.3 gather_fusion.6
  (79 shorter events, 61.7 us)
Async XLA Ops:
  10.7 14.6 %all-to-all-start = ((s32[32,1,258]{2,1,0:T(1,128)}), s32[32,1,258]{2,1,0:T(1,128)S(1)}, u32[]{:S(2)}, u32[]{:S(2)}) async-start(s32[32,1,258]{2,1,0:T(1,128)} %broadcast_in_dim.85), calls=%async_computation | async-start | bytes 98304 | tf_op jit(solution)/shard_map/all_to_all | solution.py:46
  18.0 141.0 %all-gather.9.cloned.1.call-start = ((), (), s32[]{:S(2)}) async-start(), calls=%async_computation.9 | async-start | bytes 7077888 | tf_op jit(solution)/shard_map/all_gather | solution.py:105
  25.3 0.6 copy-start.3
  43.2 63.0 %all-to-all-start.1 = ((bf16[32,4,24,256]{3,2,1,0:T(8,128)(2,1)}), bf16[32,4,24,256]{3,2,1,0:T(8,128)(2,1)S(1)}, u32[]{:S(2)}, u32[]{:S(2)}) async-start(bf16[32,4,24,256]{3,2,1,0:T(8,128)(2,1)} %bitcast.1), calls=%async_computation.1 | async-start | bytes 3145728 | tf_op jit(solution)/shard_map/all_to_all | solution.py:108
  45.9 5.1 copy-start.1
  106.2 1.1 copy-start
  160.5 32.5 %collective-permute-start = (bf16[3,768,256]{1,2,0:T(8,128)(2,1)}, bf16[3,768,256]{1,2,0:T(8,128)(2,1)}, u32[]{:S(2)}, u32[]{:S(2)}) collective-permute-start(bf16[3,768,256]{1,2,0:T(8,128)(2,1)} %copy.92), channel_id=1, source_target_pairs={{0,8},{8,16},{16,24},{24,0},{1,9},{9,17},{17,25},{25,1},{2,10},{10... | collective-permute-start | bytes 3538952 | tf_op jit(solution)/shard_map/ppermute | solution.py:126
  160.5 107.5 %all-to-all-start.2 = ((f32[32,4,24,256]{3,2,1,0:T(8,128)}), f32[32,4,24,256]{3,2,1,0:T(8,128)}, u32[]{:S(2)}, u32[]{:S(2)}) async-start(f32[32,4,24,256]{3,2,1,0:T(8,128)} %bitcast.91), calls=%async_computation.2 | async-start | bytes 6291456 | tf_op jit(solution)/shard_map/all_to_all | solution.py:121
  164.1 98.0 %all-gather.5.cloned.1.call-start = ((), (), s32[]{:S(2)}) async-start(), calls=%async_computation.6 | async-start | bytes 1966080 | tf_op jit(solution)/shard_map/all_gather | solution.py:157
  193.1 24.3 %collective-permute-start.1 = (bf16[3,768,256]{1,2,0:T(8,128)(2,1)}, bf16[3,768,256]{1,2,0:T(8,128)(2,1)}, u32[]{:S(2)}, u32[]{:S(2)}) collective-permute-start(bf16[3,768,256]{1,2,0:T(8,128)(2,1)} %collective-permute-done), channel_id=1, source_target_pairs={{0,8},{8,16},{16,24},{24,0},{1,9},{9,17},{17,25},{25,1},{2,10},{10... | collective-permute-start | bytes 3538952 | tf_op jit(solution)/shard_map/ppermute | solution.py:126
  217.3 26.7 %collective-permute-start.2 = (bf16[3,768,256]{1,2,0:T(8,128)(2,1)}, bf16[3,768,256]{1,2,0:T(8,128)(2,1)}, u32[]{:S(2)}, u32[]{:S(2)}) collective-permute-start(bf16[3,768,256]{1,2,0:T(8,128)(2,1)} %collective-permute-done.1), channel_id=1, source_target_pairs={{0,8},{8,16},{16,24},{24,0},{1,9},{9,17},{17,25},{25,1},{2,10},{10... | collective-permute-start | bytes 3538952 | tf_op jit(solution)/shard_map/ppermute | solution.py:126
  219.7 168.0 %reduce-scatter.2.cloned.1.call-start = ((), (), s32[]{:S(2)}) async-start(), calls=%async_computation.7 | async-start | bytes 7077888 | tf_op jit(solution)/shard_map/reduce_scatter | solution.py:168
  247.3 1.8 copy-start.2
  268.0 290.1 %all-gather.7.cloned.1.call-start = ((), (), s32[]{:S(2)}) async-start(), calls=%async_computation.8 | async-start | bytes 7077888 | tf_op jit(solution)/shard_map/all_gather | solution.py:175
  389.2 13.1 %copy-start.4 = (f32[3072]{0:T(1024)S(1)}, f32[3072]{0:T(1024)}, u32[]{:S(2)}) copy-start(f32[3072]{0:T(1024)} %param.18) | copy-start | bytes 36868
  404.9 166.0 %all-to-all-start.3 = ((f32[32,4,24,256]{3,2,1,0:T(8,128)}), f32[32,4,24,256]{3,2,1,0:T(8,128)}, u32[]{:S(2)}, u32[]{:S(2)}) async-start(f32[32,4,24,256]{3,2,1,0:T(8,128)} %bitcast.90), calls=%async_computation.3 | async-start | bytes 6291456 | tf_op jit(solution)/shard_map/all_to_all | solution.py:167
  570.8 22.3 %all-to-all-start.4 = ((f32[8,3,128]{2,1,0:T(4,128)}), f32[8,3,128]{2,1,0:T(4,128)S(1)}, u32[]{:S(2)}, u32[]{:S(2)}) async-start(f32[8,3,128]{2,1,0:T(4,128)} %maximum_bitcast_fusion), calls=%async_computation.5 | async-start | bytes 32768 | tf_op jit(solution)/shard_map/all_to_all | solution.py:62
Sparse Core Ops, SparseCore 0:
  36.4 122.5 all-gather.8
  268.1 119.5 reduce-scatter.1
  405.0 153.0 all-gather.6
Sparse Core Ops, SparseCore 1:
  219.8 28.1 all-gather.4
